TPU v7x, 128 devices: a whole 4x4x4 slice. The times are simulated.
128 devices in a mesh: lat: 32 (over x, y, core), lon: 4 (over z).
Axes of the slice: x: 4, y: 4, z: 4, core: 2. Of those that a mesh axis runs over, the one named last changes fastest.
Arguments:
- coeffs_old: float32 [640, 2, 3, 50, 640], P(('lat', 'lon')), may hold values from -0.16 to 0.16
- noise: bfloat16 [640, 2, 3, 50, 640], P(('lat', 'lon')), may hold values from -6 to 6
- legendre: float32 [640, 640, 640], P(('lat', 'lon')), may hold values from -0.25 to 0.25
- decay: float32 [3], replicated, may hold values from 0.3 to 0.97
- amplitude: float32 [3, 640], replicated, may hold values from 0.005 to 0.05
- wavenumber_of_slot: int32 [640], replicated, may hold values from 0 to 639, as said below
- lat_order: int32 [640], replicated, may hold values from 0 to 639, each once
Outputs:
- coeffs_new: float32 [640, 2, 3, 50, 640], P(('lat', 'lon'))
- pattern: float32 [640, 50, 1280], P(('lat', 'lon'))
Inputs may be any that keep to these rules, and one draw needn't show every extreme that they name: `wavenumber_of_slot`: every wavenumber fills exactly one slot; the sums of the wavenumbers of one device's 5 slots differ between devices by less than 128. `lat_order`: every latitude stands in exactly one row.
All inputs are finite; a program needn't handle non-finite values.
Results may differ from a plain program's by a relative error of at most 0.0003.
Values sent between devices are 32-bit elements; how exact they have to be, the bound alone decides.
A program may use at most 128 MiB of HBM per device.

v0:
```python
import jax
import jax.numpy as jnp
from jax import lax
from jax.sharding import PartitionSpec as P

LON = 1280


TWO_PI = 6.283185307179586


def evolve(coeffs_old, noise, decay, amplitude, waves):
    width = coeffs_old.shape[4]
    offsets = lax.broadcasted_iota(jnp.int32, (waves.shape[0], width), 1)
    live = waves[:, None] + offsets < width
    padded = jnp.concatenate([amplitude, jnp.zeros_like(amplitude)], axis=1)
    spread = jax.vmap(lambda wave: lax.dynamic_slice_in_dim(padded, wave, width, 1))(waves)
    factor = jnp.sqrt(1.0 - decay * decay)
    fresh = decay[None, None, :, None, None] * coeffs_old + (spread * factor[None, :, None])[
        :, None, :, None, :
    ] * noise.astype(jnp.float32)
    return jnp.where(live[:, None, None, None, :], fresh, jnp.zeros_like(fresh))


def synthesis_table(waves, length):
    column = lax.broadcasted_iota(jnp.int32, (waves.shape[0], length), 1)
    phase = waves[:, None] * column % length
    angle = phase.astype(jnp.float32) * (TWO_PI / length)
    weight = jnp.where(waves == 0, 1.0, 2.0).astype(jnp.float32)[:, None]
    return jnp.stack([weight * jnp.cos(angle), -weight * jnp.sin(angle)], axis=1)


def synthesize(values, table):
    return jnp.einsum("sreq,srl->qel", values, table, precision=lax.Precision.HIGHEST)


def local(coeffs_old, noise, legendre, decay, amplitude, wavenumber_of_slot, lat_order):
    lat_count = lax.axis_size("lat")
    lon_count = lax.axis_size("lon")
    lat_index = lax.axis_index("lat")
    lon_index = lax.axis_index("lon")
    slots = coeffs_old.shape[0]
    mine = lax.dynamic_slice_in_dim(
        wavenumber_of_slot, (lat_index * lon_count + lon_index) * slots, slots
    )
    coeffs_new = evolve(coeffs_old, noise, decay, amplitude, mine)
    field = jnp.einsum("srkej,slj->srel", coeffs_new, legendre, precision=lax.Precision.HIGHEST)
    field = jnp.take(field, lat_order, axis=3)
    ordered = wavenumber_of_slot.reshape(lat_count, lon_count, slots).transpose(1, 0, 2).reshape(-1)
    full_table = synthesis_table(ordered, LON)
    pattern = synthesize(
        lax.all_to_all(
            lax.all_to_all(field, "lat", split_axis=3, concat_axis=0, tiled=True),
            "lon",
            split_axis=3,
            concat_axis=0,
            tiled=True,
        ),
        full_table,
    )
    return (coeffs_new, pattern)


def solution(mesh):
    in_specs = (
        P(("lat", "lon"), None, None, None, None),
        P(("lat", "lon"), None, None, None, None),
        P(("lat", "lon"), None, None),
        P(),
        P(),
        P(),
        P(),
    )
    out_specs = (P(("lat", "lon"), None, None, None, None), P(("lat", "lon"), None, None))
    return jax.shard_map(local, mesh=mesh, in_specs=in_specs, out_specs=out_specs, check_vma=False)
```

profile of v0, /device:TPU:1, one launch (start us, length us, event | category | flops | bytes accessed | tf_op | source)
XLA Modules:
  0.0 150.4 jit_solution(14142262357541582796)
XLA Ops:
  0.6 0.7 compare_and_fusion
  1.3 0.7 compare_select_fusion
  2.0 0.7 subtract_sqrt_fusion
  2.7 0.8 fusion.12
  3.5 0.7 concatenate.6
  4.2 6.6 %while.1 = (s32[]{:T(128)}, f32[3,1280]{1,0:T(4,128)S(1)}, s32[5,2]{0,1:T(2,128)S(1)}, f32[5,3,640]{2,1,0:T(4,128)S(1)}, s32[]{:T(128)}) while((s32[]{:T(128)}, f32[3,1280]{1,0:T(4,128)S(1)}, s32[5,2]{0,1:T(2,128)S(1)}, f32[5,3,640]{2,1,0:T(4,128)S(1)}, s32[]{:T(128)}) %tuple.24), condition=%wide.while_cond, body=%wide.while_body.sunk | while | flops 2 | bytes 20585 | solution.py:17
  4.8 0.7 bitcast_dynamic-update-slice_fusion.2
  5.6 0.5 slice.14
  6.2 0.7 bitcast_dynamic-update-slice_fusion.2
  7.0 0.5 slice.14
  7.5 0.7 bitcast_dynamic-update-slice_fusion.2
  8.3 0.5 slice.14
  8.8 0.7 bitcast_dynamic-update-slice_fusion.2
  10.1 0.7 bitcast_dynamic-update-slice_fusion.2
  10.9 9.0 %fusion.15 = (f32[5,2,50,640]{3,1,2,0:T(2,128)S(1)}, f32[5,2,3,50,640]{4,1,3,2,0:T(2,128)}) fusion(bf16[5,2,3,50,640]{4,1,3,2,0:T(2,128)(2,1)} %param.8, f32[5,3,640]{2,1,0:T(4,128)S(1)} %broadcast_multiply_fusion, f32[5,2,3,50,640]{4,1,3,2,0:T(2,128)} %param.7, f32[3]{0:T(128)} %param.10, pred[5,640]{1,0:T(8,128)(4,1)S(1)} %add_compare_fusion), kind=kLoop, calls=%fused_computation.33 | loop fusion | flops 5440000 | bytes 10921612 | tf_op jit(solution)/shard_map/srkej,slj->srel/reduce_sum | solution.py:47
  19.9 9.3 %fusion = f32[5,2,50,640]{3,2,1,0:T(8,128)} fusion(f32[5,640,640]{2,1,0:T(8,128)S(1)} %copy-done, f32[5,2,50,640]{3,1,2,0:T(2,128)S(1)} %get-tuple-element.18), kind=kOutput, calls=%fused_computation.3 | convolution fusion | flops 2457600000 | bytes 10752000 | tf_op jit(solution)/shard_map/srkej,slj->srel/dot_general | solution.py:47
  29.2 3.8 %copy.18 = f32[5,2,50,640]{2,1,3,0:T(2,128)S(1)} copy(f32[5,2,50,640]{3,2,1,0:T(8,128)} %fusion) | data formatting | bytes 2560000 | tf_op jit(solution)/shard_map/srkej,slj->srel/dot_general | solution.py:47
  33.0 7.3 %gather_fusion = f32[640,5,2,50]{3,2,1,0:T(2,128)} fusion(f32[5,2,50,640]{2,1,3,0:T(2,128)S(1)} %copy.18, s32[1024]{0:T(1024)S(1)} %pad_clamp_fusion), kind=kCustom, calls=%fused_computation | custom fusion | bytes 2562560 | tf_op jit(solution)/shard_map/jit(_take)/gather | solution.py:48
  40.3 4.2 %fusion.16 = f32[640,5,2,50]{3,2,1,0:T(2,128)S(1)} fusion(f32[640,5,2,50]{3,2,1,0:T(2,128)} %gather_fusion, pred[640]{0:T(1024)(128)(4,1)S(1)} %compare_and_fusion), kind=kLoop, calls=%fused_computation.34 | loop fusion | flops 320000 | bytes 2560640
  44.6 6.6 %reshape.218 = f32[32,1,10000]{2,1,0:T(1,128)} reshape(f32[640,5,2,50]{3,2,1,0:T(2,128)S(1)} %fusion.16) | data formatting | bytes 2560000
  51.1 28.6 %all_to_all.36 = f32[32,1,10000]{2,1,0:T(1,128)S(1)} all-to-all(f32[32,1,10000]{2,1,0:T(1,128)} %reshape.218), channel_id=1, replica_groups=mesh['lat'=32,'lon'=4] {'lat'}, dimensions={0} | all-to-all | bytes 2560000 | tf_op jit(solution)/shard_map/all_to_all | solution.py:53
  79.7 0.5 broadcast.203
  80.3 5.0 %reduce = f32[32,10000]{1,0:T(8,128)} reduce(f32[32,1,10000]{2,1,0:T(1,128)S(1)} %all_to_all.36, f32[]{:T(128)} %broadcast.203), dimensions={1}, to_apply=%all_to_all.26.reduce_sub_computation | reduce | bytes 2560004 | tf_op jit(solution)/shard_map/all_to_all | solution.py:53
  85.3 6.7 %reshape.219 = f32[640,5,2,50]{3,2,1,0:T(2,128)S(1)} reshape(f32[32,10000]{1,0:T(8,128)} %reduce) | data formatting | bytes 2560000
  92.0 2.8 %copy.20 = f32[32,5,2,50,20]{3,2,4,1,0:T(2,128)} copy(f32[32,5,2,50,20]{3,2,1,4,0:T(2,128)S(1)} %bitcast.42) | data formatting | bytes 2560000 | tf_op jit(solution)/shard_map/all_to_all | solution.py:53
  94.8 7.7 %copy.21 = f32[160,2,50,20]{0,1,2,3:T(2,128)} copy(f32[160,2,50,20]{2,1,3,0:T(2,128)} %bitcast.43) | data formatting | bytes 2560000 | tf_op jit(solution)/shard_map/all_to_all | solution.py:53
  102.5 5.2 %all-to-all-start.1 = ((f32[160,2,50,20]{0,1,2,3:T(2,128)}), f32[160,2,50,20]{0,1,2,3:T(2,128)}, u32[]{:S(2)}, u32[]{:S(2)}) async-start(f32[160,2,50,20]{0,1,2,3:T(2,128)} %copy.21), calls=%async_computation.1 | async-start | bytes 4096000 | tf_op jit(solution)/shard_map/all_to_all | solution.py:52
  108.1 15.2 %cosine_multiply_fusion = (f32[640,1,1280]{2,0,1:T(8,128)S(1)}, f32[640,1,1280]{2,0,1:T(8,128)}) fusion(s32[640]{0:T(1024)S(1)} %reshape.185, f32[640]{0:T(1024)S(1)} %get-tuple-element.24, f32[640]{0:T(1024)S(1)} %get-tuple-element.25), kind=kLoop, calls=%fused_computation.15 | loop fusion | flops 9011200 | bytes 6561280 | tf_op jit(solution)/shard_map/mul | solution.py:30
  123.3 10.4 %all-to-all-done.1 = f32[160,2,50,20]{0,1,2,3:T(2,128)} async-done(((f32[160,2,50,20]{0,1,2,3:T(2,128)}), f32[160,2,50,20]{0,1,2,3:T(2,128)}, u32[]{:S(2)}, u32[]{:S(2)}) %all-to-all-start.1) | async-done | bytes 1280032 | tf_op jit(solution)/shard_map/all_to_all | solution.py:52
  133.7 3.5 %copy.29 = f32[4,160,2,50,5]{1,0,3,2,4:T(4,128)} copy(f32[4,160,2,50,5]{1,2,3,4,0:T(2,128)} %bitcast.12) | data formatting | bytes 2560000 | tf_op jit(solution)/shard_map/all_to_all | solution.py:52
  137.1 3.6 %reshape.217 = f32[640,2,50,5]{0,2,1,3:T(8,128)} reshape(f32[4,160,2,50,5]{1,0,3,2,4:T(4,128)} %copy.29) | data formatting | bytes 2560000 | tf_op jit(solution)/shard_map/all_to_all | solution.py:52
  140.7 9.8 %fusion.10 = f32[5,50,1280]{2,1,0:T(8,128)} fusion(f32[640,2,50,5]{0,2,1,3:T(8,128)} %reshape.217, f32[640,1,1280]{2,0,1:T(8,128)} %get-tuple-element.23, f32[640,1,1280]{2,0,1:T(8,128)S(1)} %get-tuple-element.22), kind=kOutput, calls=%fused_computation.20 | convolution fusion | flops 4916838400 | bytes 9113600 | tf_op jit(solution)/shard_map/sreq,srl->qel/dot_general | solution.py:34
  (20 shorter events, 2.0 us)
Async XLA Ops:
  10.9 9.0 %copy-start = (f32[5,640,640]{2,1,0:T(8,128)S(1)}, f32[5,640,640]{2,1,0:T(8,128)}, u32[]{:S(2)}) copy-start(f32[5,640,640]{2,1,0:T(8,128)} %param.9) | copy-start | bytes 24576004
  102.5 5.2 %copy-start.1 = (s32[640]{0:T(1024)S(1)}, s32[640]{0:T(1024)}, u32[]{:S(2)}) copy-start(s32[640]{0:T(1024)} %param.12) | copy-start | bytes 7684
  102.5 31.2 %all-to-all-start.1 = ((f32[160,2,50,20]{0,1,2,3:T(2,128)}), f32[160,2,50,20]{0,1,2,3:T(2,128)}, u32[]{:S(2)}, u32[]{:S(2)}) async-start(f32[160,2,50,20]{0,1,2,3:T(2,128)} %copy.21), calls=%async_computation.1 | async-start | bytes 4096000 | tf_op jit(solution)/shard_map/all_to_all | solution.py:52
where the time goes:
time: 151 us; the launch traced here: 150 us
  local copies, waits for them, and re-layouts  50.1 us (33%)
  other arithmetic  36.4 us (24%)
  blocking collectives  28.6 us (19%)
  matrix products  19 us (13%)
  waiting for transfers between devices  10.4 us (7%)
  starting transfers between devices  5.16 us (3%)
    all_to_all x1, blocking collectives, local(): lax.all_to_all(field, 'lat', split_axis=3, concat_axis=0, tiled=True)  28.6 us
    mul x1, other arithmetic, synthesis_table(): weight * jnp.cos(angle)  15.2 us
    unnamed x6, local copies, waits for them, and re-layouts  13.2 us
    all_to_all x3, local copies, waits for them, and re-layouts, local(): lax.all_to_all(field, 'lat', split_axis=3, concat_axis=0, tiled=True)  11 us
    all_to_all x1, waiting for transfers between devices, local(): lax.all_to_all(lax.all_to_all(field, 'lat', split_axis=3, concat_axis=0,...  10.4 us
    dot_general x1, matrix products, synthesize(): jnp.einsum('sreq,srl->qel', values, table, precision=lax.Precision.HIGHEST)  9.76 us
    dot_general x1, matrix products, local(): jnp.einsum('srkej,slj->srel', coeffs_new, legendre, precision=lax.Precisi...  9.27 us
    reduce_sum x1, other arithmetic, local(): jnp.einsum('srkej,slj->srel', coeffs_new, legendre, precision=lax.Precisi...  9 us
  transfers between devices with their start and end apart: 1, of which 1 were waited for; matrix products, arithmetic and copies ran while one was open for 10% of the time, Pallas kernels for 0%

commit v1 on v0

v1 whole, which is shorter than its diff:
```python
import functools

import jax
import jax.numpy as jnp
from jax import lax
from jax.experimental import pallas as pl
from jax.experimental.pallas import tpu as pltpu
from jax.sharding import PartitionSpec as P

MESH = pl.DeviceIdType.MESH
LON = 1280
HALF = LON // 2
TWO_PI = 6.283185307179586
SLOTS = 5
DEVS = 128
ROWS = 5
MEMBERS = 50
WIDTH = 640
SCALES = 3
F32 = jnp.float32
BF16 = jnp.bfloat16


def evolve_kernel(waves_ref, decay_ref, amp_ref, old_ref, noise_ref, new_ref, sum_ref):
    s = pl.program_id(0)
    me = lax.axis_index("lat") * 4 + lax.axis_index("lon")
    wave = waves_ref[me * SLOTS + s]
    lane = lax.broadcasted_iota(jnp.int32, (1, WIDTH), 1)
    live = lane < WIDTH - wave
    shifted = pltpu.roll(amp_ref[...], lax.rem(WIDTH - wave, WIDTH), 1)
    keep, gain = [], []
    for k in range(SCALES):
        d = jnp.full((1, WIDTH), decay_ref[k], F32)
        keep.append(jnp.where(live, d, 0.0))
        gain.append(jnp.where(live, shifted[k : k + 1] * jnp.sqrt(1.0 - d * d), 0.0))
    for e in range(MEMBERS):
        total = None
        for k in range(SCALES):
            fresh = keep[k] * old_ref[0, k, e] + gain[k] * noise_ref[0, k, e].astype(F32)
            new_ref[0, k, e] = fresh
            total = fresh if total is None else total + fresh
        sum_ref[0, e : e + 1, :] = total[0:1]
        sum_ref[0, MEMBERS + e : MEMBERS + e + 1, :] = total[1:2]


def evolve(waves, decay, amplitude, old, noise):
    block = pl.BlockSpec((1, SCALES, MEMBERS, 2, WIDTH), lambda s: (s, 0, 0, 0, 0))
    return pl.pallas_call(
        evolve_kernel,
        name="evolve",
        grid=(SLOTS,),
        out_shape=(
            jax.ShapeDtypeStruct((SLOTS, SCALES, MEMBERS, 2, WIDTH), F32),
            jax.ShapeDtypeStruct((SLOTS, 2 * MEMBERS, WIDTH), F32),
        ),
        in_specs=[
            pl.BlockSpec(memory_space=pltpu.SMEM),
            pl.BlockSpec(memory_space=pltpu.SMEM),
            pl.BlockSpec(memory_space=pltpu.VMEM),
            block,
            block,
        ],
        out_specs=(block, pl.BlockSpec((1, 2 * MEMBERS, WIDTH), lambda s: (s, 0, 0))),
        compiler_params=pltpu.CompilerParams(dimension_semantics=("arbitrary",)),
    )(waves, decay, amplitude, old, noise)


def offsets():
    out = []
    for dx in range(4):
        for dy in range(4):
            for dz in range(4):
                for dc in range(2):
                    if dx or dy or dz or dc:
                        hops = sum(min(d, 4 - d) for d in (dx, dy, dz))
                        out.append((-hops, dx, dy, dz, dc))
    return [o[1:] for o in sorted(out)]


def split(x):
    hi = x.astype(BF16)
    return hi, (x - hi.astype(F32)).astype(BF16)


def dot(a, b, dims=(((1,), (0,)), ((), ()))):
    return lax.dot_general(a, b, dims, preferred_element_type=F32)


def unit(turns):
    near = jnp.round(turns * (1.0 / LON))
    x = (turns - near * LON) * (TWO_PI / LON)
    y = x * x
    c, s = None, None
    for n in range(8, -1, -1):
        a = (-1.0) ** n
        fact = 1.0
        for i in range(1, 2 * n + 1):
            fact *= i
        c = a / fact if c is None else c * y + a / fact
        s = a / (fact * (2 * n + 1)) if s is None else s * y + a / (fact * (2 * n + 1))
    return c, s * x


def exchange_kernel(
    order_ref, waves_ref, sum_hbm, leg_hbm, out_ref,
    coef, leg, perm, send, recv, tab_hi, tab_lo, acc,
    coef_sem, leg_sem, send_sem, recv_sem,
):
    lat = lax.axis_index("lat")
    z = lax.axis_index("lon")
    me = lat * 4 + z
    x, y, c = lat // 8, lax.rem(lat // 2, 4), lax.rem(lat, 2)

    def peer(o):
        dx, dy, dz, dc = o
        px, py, pz = lax.rem(x + dx, 4), lax.rem(y + dy, 4), lax.rem(z + dz, 4)
        pc = lax.rem(c + dc, 2)
        return (px * 4 + py) * 2 + pc, pz

    barrier = pltpu.get_barrier_semaphore()
    peers = [peer(o) for o in offsets()]
    for p in peers:
        pl.semaphore_signal(barrier, inc=1, device_id=p, device_id_type=MESH)
    loads = []
    for s in range(SLOTS):
        a = pltpu.make_async_copy(sum_hbm.at[s], coef.at[s], coef_sem.at[s])
        b = pltpu.make_async_copy(leg_hbm.at[s], leg.at[s], leg_sem.at[s])
        a.start()
        b.start()
        loads.append((a, b))

    lane = lax.broadcasted_iota(jnp.int32, (DEVS, WIDTH), 1)
    row = lax.broadcasted_iota(jnp.int32, (DEVS, WIDTH), 0)
    order = order_ref[...]
    for q in range(ROWS):
        mine = jnp.where(lane == row * ROWS + q, order, 0)
        shown = jnp.sum(mine.astype(F32), axis=1, keepdims=True).astype(jnp.int32)
        perm[q * DEVS : (q + 1) * DEVS, :] = jnp.where(lane == shown, 1.0, 0.0).astype(BF16)

    lanes = lax.broadcasted_iota(jnp.int32, (DEVS, 128), 1)
    nt = (((1,), (1,)), ((), ()))

    def field(s):
        for copy in loads[s]:
            copy.wait()
        c_hi, c_lo = split(coef[s])
        pad = jnp.zeros((128 - 2 * MEMBERS, WIDTH), BF16)
        c_hi = jnp.concatenate([c_hi, pad], axis=0)
        c_lo = jnp.concatenate([c_lo, pad], axis=0)
        l_hi, l_lo = split(leg[s])
        f = dot(l_hi, c_hi, nt) + (dot(l_hi, c_lo, nt) + dot(l_lo, c_hi, nt))
        f_hi, f_lo = split(f)
        p = perm[...]
        g = dot(p, f_hi) + dot(p, f_lo)
        for r in range(2):
            low, high = None, None
            for q in range(ROWS):
                block = g[q * DEVS : (q + 1) * DEVS]
                shift = ((q - r) * MEMBERS) % 128
                if shift:
                    block = pltpu.roll(block, shift, 1)
                start = q * MEMBERS
                if start < 128:
                    low = block if low is None else jnp.where(lanes >= start, block, low)
                if start + MEMBERS > 128:
                    high = block if high is None else jnp.where(lanes >= start - 128, block, high)
            send[s, :, 2 * r, :] = low
            send[s, :, 2 * r + 1, :] = high

    def start(s):
        for p in peers:
            pltpu.make_async_remote_copy(
                src_ref=send.at[s, p[0] * 4 + p[1]],
                dst_ref=recv.at[s, me],
                send_sem=send_sem.at[s],
                recv_sem=recv_sem.at[s],
                device_id=p,
                device_id_type=MESH,
            ).start()
        recv[s, pl.ds(me, 1)] = send[s, pl.ds(me, 1)]

    field(0)
    pl.semaphore_wait(barrier, DEVS - 1)
    start(0)
    for s in range(1, SLOTS):
        field(s)
        start(s)

    waves = waves_ref[...]
    signs = []
    for s in range(SLOTS):
        mine = jnp.where(lane == row * SLOTS + s, waves, 0)
        m = jnp.sum(mine.astype(F32), axis=1, keepdims=True)
        m = jnp.broadcast_to(m, (DEVS, 128))
        weight = jnp.where(m == 0.0, 1.0, 2.0)
        cos, sin = unit(m * lanes.astype(F32))
        step_c, step_s = unit(m * 128.0)
        cos, sin = weight * cos, -weight * sin
        for a in range(HALF // 128):
            hi, lo = split(cos)
            tab_hi[s, 0:DEVS, a * 128 : (a + 1) * 128] = hi
            tab_lo[s, 0:DEVS, a * 128 : (a + 1) * 128] = lo
            hi, lo = split(sin)
            tab_hi[s, DEVS:, a * 128 : (a + 1) * 128] = hi
            tab_lo[s, DEVS:, a * 128 : (a + 1) * 128] = lo
            cos, sin = cos * step_c + sin * step_s, sin * step_c - cos * step_s
        odd = m - 2.0 * jnp.floor(m * 0.5)
        sign = (1.0 - 2.0 * odd).T
        signs.append(jnp.concatenate([sign[0:1], sign[0:1]], axis=1).astype(F32))

    for s in range(SLOTS):
        whole = recv.at[s, pl.ds(0, DEVS - 1)]
        pltpu.make_async_copy(whole, whole, recv_sem.at[s]).wait()
        rows = []
        for lt in range(2):
            got = jnp.concatenate([recv[s, :, 2 * r + lt, :] for r in range(2)], axis=0)
            rows.append(got.T)
        w = jnp.concatenate(rows, axis=0)
        w_hi, w_lo = split(w)
        sg = signs[s].astype(BF16)
        left_hi = jnp.concatenate([w_hi, w_hi * sg], axis=0)
        left_lo = jnp.concatenate([w_lo, w_lo * sg], axis=0)
        t_hi, t_lo = tab_hi[s], tab_lo[s]
        part = dot(left_hi, t_hi) + (dot(left_lo, t_hi) + dot(left_hi, t_lo))
        if s == 0:
            acc[...] = part
        else:
            acc[...] += part
    for q in range(ROWS):
        for h in range(2):
            base = h * 256 + q * MEMBERS
            out_ref[q, :, h * HALF : (h + 1) * HALF] = acc[base : base + MEMBERS, :]
    for s in range(SLOTS):
        whole = send.at[s, pl.ds(0, DEVS - 1)]
        pltpu.make_async_copy(whole, whole, send_sem.at[s]).wait()


def exchange(order, waves, summed, legendre):
    return pl.pallas_call(
        exchange_kernel,
        name="exchange",
        out_shape=jax.ShapeDtypeStruct((ROWS, MEMBERS, LON), F32),
        in_specs=[
            pl.BlockSpec(memory_space=pltpu.VMEM),
            pl.BlockSpec(memory_space=pltpu.VMEM),
            pl.BlockSpec(memory_space=pl.ANY),
            pl.BlockSpec(memory_space=pl.ANY),
        ],
        out_specs=pl.BlockSpec(memory_space=pltpu.VMEM),
        scratch_shapes=[
            pltpu.VMEM((SLOTS, 2 * MEMBERS, WIDTH), F32),
            pltpu.VMEM((SLOTS, WIDTH, WIDTH), F32),
            pltpu.VMEM((WIDTH, WIDTH), BF16),
            pltpu.VMEM((SLOTS, DEVS, 4, 128), F32),
            pltpu.VMEM((SLOTS, DEVS, 4, 128), F32),
            pltpu.VMEM((SLOTS, 2 * DEVS, HALF), BF16),
            pltpu.VMEM((SLOTS, 2 * DEVS, HALF), BF16),
            pltpu.VMEM((512, HALF), F32),
            pltpu.SemaphoreType.DMA((SLOTS,)),
            pltpu.SemaphoreType.DMA((SLOTS,)),
            pltpu.SemaphoreType.DMA((SLOTS,)),
            pltpu.SemaphoreType.DMA((SLOTS,)),
        ],
        compiler_params=pltpu.CompilerParams(collective_id=0, has_side_effects=True, vmem_limit_bytes=48 * 2**20),
    )(order, waves, summed, legendre)


def local(coeffs_old, noise, legendre, decay, amplitude, wavenumber_of_slot, lat_order):
    old = coeffs_old.transpose(0, 2, 3, 1, 4)
    fresh = noise.transpose(0, 2, 3, 1, 4)
    new, summed = evolve(wavenumber_of_slot, decay, amplitude, old, fresh)
    pattern = exchange(lat_order.reshape(1, -1), wavenumber_of_slot.reshape(1, -1), summed, legendre)
    return new.transpose(0, 3, 1, 2, 4), pattern


def solution(mesh):
    split_slots = P(("lat", "lon"), None, None, None, None)
    in_specs = (split_slots, split_slots, P(("lat", "lon"), None, None), P(), P(), P(), P())
    out_specs = (split_slots, P(("lat", "lon"), None, None))
    return jax.shard_map(local, mesh=mesh, in_specs=in_specs, out_specs=out_specs, check_vma=False)
```

time: 151 us -> 42.3 us (0.28)
  local copies, waits for them, and re-layouts: 50.1 us -> 3.8 us
  Pallas kernels: 0 us -> 37.5 us
  other arithmetic: 36.4 us -> 0 us
  blocking collectives: 28.6 us -> 0 us
  matrix products: 19 us -> 0 us
  waiting for transfers between devices: 10.4 us -> 0 us
  starting transfers between devices: 5.16 us -> 0 us
    pallas_call x0 -> x2, Pallas kernels: none -> 37.5 us  [the longest x1 29.4 us: exchange(): pl.pallas_call(exchange_kernel, name='exchange', out_shape=jax.ShapeDtype...]
    all_to_all x1 -> x0, blocking collectives: 28.6 us -> none  [local(): lax.all_to_all(field, 'lat', split_axis=3, concat_axis=0, tiled=True)]
    dot_general x2 -> x0, matrix products: 19 us -> none  [the longest x1 9.76 us: synthesize(): jnp.einsum('sreq,srl->qel', values, table, precision=lax.Precision.HIGHEST)]
    all_to_all x5 -> x0, local copies, waits for them, and re-layouts: 18 us -> none  [the longest x3 11 us: local(): lax.all_to_all(field, 'lat', split_axis=3, concat_axis=0, tiled=True)]
    mul x2 -> x0, other arithmetic: 15.3 us -> none  [the longest x1 15.2 us: synthesis_table(): weight * jnp.cos(angle)]
    gather x16 -> x0, local copies, waits for them, and re-layouts: 13.9 us -> none  [the longest x1 7.33 us: local(): field = jnp.take(field, lat_order, axis=3)]
    unnamed x6 -> x3, local copies, waits for them, and re-layouts: 13.2 us -> 2.42 us
    all_to_all x1 -> x0, waiting for transfers between devices: 10.4 us -> none  [local(): lax.all_to_all(lax.all_to_all(field, 'lat', split_axis=3, concat_axis=0,...]
  transfers between devices with their start and end apart: 1 -> 0, of which waited for: 1 -> 0; matrix products, arithmetic and copies ran while one was open for 10% -> 0% of each run, Pallas kernels for 0% -> 0%
where the time goes in v1:
time: 42.3 us; the launch traced here: 42 us
  Pallas kernels  37.5 us (89%)
  local copies, waits for them, and re-layouts  3.8 us (9%)
  between operations  0.64 us (2%)
    pallas_call x1, Pallas kernels, exchange(): pl.pallas_call(exchange_kernel, name='exchange', out_shape=jax.ShapeDtype...  29.4 us
    pallas_call x1, Pallas kernels, evolve(): pl.pallas_call(evolve_kernel, name='evolve', grid=(SLOTS,), out_shape=(ja...  8.11 us
    unnamed x3, local copies, waits for them, and re-layouts  2.42 us

profile of v1, /device:TPU:1, one launch (start us, length us, event | category | flops | bytes accessed | tf_op | source)
XLA Modules:
  0.0 42.0 jit_solution(6955632946494290909)
XLA Ops:
  0.6 0.7 %reshape.10.order_ref = s32[1,640]{1,0:T(1,128)S(1)} reshape(s32[640]{0:T(1024)} %param.13) | data formatting | bytes 5120 | tf_op jit(solution)/shard_map/reshape | solution.py:272
  1.3 0.7 %reshape.11.waves_ref = s32[1,640]{1,0:T(1,128)S(1)} reshape(s32[640]{0:T(1024)} %waves_ref.1) | data formatting | bytes 5120 | tf_op jit(solution)/shard_map/reshape | solution.py:272
  2.0 8.1 %evolve.1 = (f32[5,3,50,2,640]{4,3,2,1,0:T(2,128)}, f32[5,100,640]{2,1,0:T(8,128)}) custom-call(s32[640]{0:T(1024)} %waves_ref.1, f32[3]{0:T(128)} %decay_ref.1, f32[3,640]{1,0:T(4,128)} %amp_ref.1, f32[5,3,50,2,640]{4,3,2,1,0:T(2,128)} %bitcast.3, bf16[5,3,50,2,640]{4,3,2,1,0:T(2,128)(2,1)} %bitcast.4), custom_call_target="tpu_custom_call" | custom-call | tf_op jit(solution)/shard_map/evolve/pallas_call | solution.py:48
  10.1 0.0 copy-start
  10.1 1.3 %copy-done = f32[5,100,640]{2,1,0:T(8,128)S(1)} copy-done((f32[5,100,640]{2,1,0:T(8,128)S(1)}, f32[5,100,640]{2,1,0:T(8,128)}, u32[]{:S(2)}) %copy-start) | copy-done | bytes 1280024
  11.4 29.4 %exchange.1 = f32[5,50,1280]{2,1,0:T(8,128)S(1)} custom-call(s32[1,640]{1,0:T(1,128)S(1)} %reshape.10.order_ref, s32[1,640]{1,0:T(1,128)S(1)} %reshape.11.waves_ref, f32[5,100,640]{2,1,0:T(8,128)S(1)} %copy-done, f32[5,640,640]{2,1,0:T(8,128)} %leg_hbm.1), custom_call_target="tpu_custom_call" | custom-call | tf_op jit(solution)/shard_map/exchange/pallas_call | solution.py:239
  40.9 1.1 %copy.10 = f32[5,50,1280]{2,1,0:T(8,128)} copy(f32[5,50,1280]{2,1,0:T(8,128)S(1)} %exchange.1) | data formatting | bytes 2560000
Async XLA Ops:
  10.1 1.3 %copy-start = (f32[5,100,640]{2,1,0:T(8,128)S(1)}, f32[5,100,640]{2,1,0:T(8,128)}, u32[]{:S(2)}) copy-start(f32[5,100,640]{2,1,0:T(8,128)} %get-tuple-element.5.sum_hbm) | copy-start | bytes 3840004

commit v2 on v1

v2 whole, which is shorter than its diff:
```python
import functools

import jax
import jax.numpy as jnp
from jax import lax
from jax.experimental import pallas as pl
from jax.experimental.pallas import tpu as pltpu
from jax.sharding import PartitionSpec as P

MESH = pl.DeviceIdType.MESH
LON = 1280
HALF = LON // 2
TWO_PI = 6.283185307179586
SLOTS = 5
DEVS = 128
ROWS = 5
MEMBERS = 50
WIDTH = 640
SCALES = 3
TILES = WIDTH // 128
F32 = jnp.float32
BF16 = jnp.bfloat16


def offsets():
    out = []
    for dx in range(4):
        for dy in range(4):
            for dz in range(4):
                for dc in range(2):
                    if dx or dy or dz or dc:
                        hops = sum(min(d, 4 - d) for d in (dx, dy, dz))
                        out.append((-hops, dx, dy, dz, dc))
    return [o[1:] for o in sorted(out)]


def split(x):
    hi = x.astype(BF16)
    return hi, (x - hi.astype(F32)).astype(BF16)


def dot(a, b, dims=(((1,), (0,)), ((), ()))):
    return lax.dot_general(a, b, dims, preferred_element_type=F32)


def unit(turns):
    near = jnp.round(turns * (1.0 / LON))
    x = (turns - near * LON) * (TWO_PI / LON)
    y = x * x
    c, s = None, None
    for n in range(8, -1, -1):
        a = (-1.0) ** n
        fact = 1.0
        for i in range(1, 2 * n + 1):
            fact *= i
        c = a / fact if c is None else c * y + a / fact
        s = a / (fact * (2 * n + 1)) if s is None else s * y + a / (fact * (2 * n + 1))
    return c, s * x


def exchange_kernel(
    order_hbm, waves_hbm, decay_hbm, amp_hbm, old_hbm, noise_hbm, leg_hbm,
    new_ref, acc_ref, last_ref, sign_ref, last_hi, last_lo,
    order_ref, waves_ref, wave_ref, decay_ref, amp_ref,
    old, noise, leg, total, coef, perm, send, recv, tab_hi, tab_lo,
    small_sem, load_sem, leg_sem, send_sem, recv_sem,
):
    lat = lax.axis_index("lat")
    z = lax.axis_index("lon")
    me = lat * 4 + z
    x, y, c = lat // 8, lax.rem(lat // 2, 4), lax.rem(lat, 2)

    def peer(o):
        dx, dy, dz, dc = o
        px, py, pz = lax.rem(x + dx, 4), lax.rem(y + dy, 4), lax.rem(z + dz, 4)
        pc = lax.rem(c + dc, 2)
        return (px * 4 + py) * 2 + pc, pz

    barrier = pltpu.get_barrier_semaphore()
    peers = [peer(o) for o in offsets()]
    for p in peers:
        pl.semaphore_signal(barrier, inc=1, device_id=p, device_id_type=MESH)

    def load(s):
        for t in range(TILES):
            lanes_of = pl.ds(t * 128, 128)
            pltpu.make_async_copy(old_hbm.at[s, :, :, :, lanes_of], old.at[s, t], load_sem.at[0, s]).start()
            pltpu.make_async_copy(noise_hbm.at[s, :, :, :, lanes_of], noise.at[s, t], load_sem.at[1, s]).start()
        pltpu.make_async_copy(leg_hbm.at[s], leg.at[s], leg_sem.at[s]).start()

    small = [
        pltpu.make_async_copy(src, dst, small_sem.at[i])
        for i, (src, dst) in enumerate(
            [
                (order_hbm, order_ref),
                (waves_hbm, waves_ref),
                (waves_hbm, wave_ref),
                (decay_hbm, decay_ref),
                (amp_hbm, amp_ref),
            ]
        )
    ]
    for copy in small:
        copy.start()
    load(0)
    load(1)
    for copy in small:
        copy.wait()

    lane = lax.broadcasted_iota(jnp.int32, (DEVS, WIDTH), 1)
    row = lax.broadcasted_iota(jnp.int32, (DEVS, WIDTH), 0)
    order = order_ref[...].reshape(1, WIDTH)
    for q in range(ROWS):
        mine = jnp.where(lane == row * ROWS + q, order, 0)
        shown = jnp.sum(mine.astype(F32), axis=1, keepdims=True).astype(jnp.int32)
        perm[q * DEVS : (q + 1) * DEVS, :] = jnp.where(lane == shown, 1.0, 0.0).astype(BF16)

    lanes = lax.broadcasted_iota(jnp.int32, (DEVS, 128), 1)
    nt = (((1,), (1,)), ((), ()))
    amp = amp_ref[...]
    coef[...] = jnp.zeros_like(coef)

    def advance(s):
        pltpu.make_async_copy(old.at[s], old.at[s], load_sem.at[0, s]).wait()
        pltpu.make_async_copy(noise.at[s], noise.at[s], load_sem.at[1, s]).wait()
        wave = wave_ref[me * SLOTS + s]
        live = lane[0:1] < WIDTH - wave
        shifted = pltpu.roll(amp, lax.rem(WIDTH - wave, WIDTH), 1)
        keep, gain = [], []
        for k in range(SCALES):
            d = jnp.full((1, WIDTH), decay_ref[k], F32)
            keep.append(jnp.where(live, d, 0.0))
            gain.append(jnp.where(live, shifted[k : k + 1] * jnp.sqrt(1.0 - d * d), 0.0))
        for t in range(TILES):
            at = slice(t * 128, (t + 1) * 128)
            summed = None
            for k in range(SCALES):
                fresh = (
                    keep[k][:, at] * old.at[s, t, k].reshape(2 * MEMBERS, 128)[...]
                    + gain[k][:, at] * noise.at[s, t, k].reshape(2 * MEMBERS, 128)[...].astype(F32)
                )
                new_ref.at[s, t, k].reshape(2 * MEMBERS, 128)[...] = fresh
                summed = fresh if summed is None else summed + fresh
            total[t, 0 : 2 * MEMBERS, :] = summed
            for r in range(2):
                coef[r * 64 : r * 64 + MEMBERS, at] = total[t, pl.ds(r, MEMBERS, stride=2), :]

    def field(s):
        advance(s)
        pltpu.make_async_copy(leg_hbm.at[s], leg.at[s], leg_sem.at[s]).wait()
        if s + 2 < SLOTS:
            load(s + 2)
        c_hi, c_lo = split(coef[...])
        l_hi, l_lo = split(leg[s])
        f = dot(l_hi, jnp.concatenate([c_hi, c_lo], axis=0), nt)
        f = f[:, 0:128] + (f[:, 128:] + dot(l_lo, c_hi, nt))
        f_hi, f_lo = split(f)
        g = dot(perm[...], jnp.concatenate([f_hi, f_lo], axis=1))
        g = g[:, 0:128] + g[:, 128:]
        for r in range(2):
            low, high = None, None
            for q in range(ROWS):
                block = g[q * DEVS : (q + 1) * DEVS]
                shift = (q * MEMBERS - r * 64) % 128
                if shift:
                    block = pltpu.roll(block, shift, 1)
                start = q * MEMBERS
                if start < 128:
                    low = block if low is None else jnp.where(lanes >= start, block, low)
                if start + MEMBERS > 128:
                    high = block if high is None else jnp.where(lanes >= start - 128, block, high)
            send[s, :, 2 * r, :] = low
            send[s, :, 2 * r + 1, :] = high

    def start(s):
        for p in peers:
            pltpu.make_async_remote_copy(
                src_ref=send.at[s, p[0] * 4 + p[1]],
                dst_ref=recv.at[s, me],
                send_sem=send_sem.at[s],
                recv_sem=recv_sem.at[s],
                device_id=p,
                device_id_type=MESH,
            ).start()
        recv[s, pl.ds(me, 1)] = send[s, pl.ds(me, 1)]

    field(0)
    pl.semaphore_wait(barrier, DEVS - 1)
    start(0)
    for s in range(1, SLOTS):
        field(s)
        start(s)

    waves = waves_ref[...].reshape(1, WIDTH)
    signs = []
    for s in range(SLOTS):
        if s < SLOTS - 1:
            t_hi, t_lo = tab_hi.at[s], tab_lo.at[s]
        else:
            t_hi, t_lo = last_hi, last_lo
        mine = jnp.where(lane == row * SLOTS + s, waves, 0)
        m = jnp.sum(mine.astype(F32), axis=1, keepdims=True)
        m = jnp.broadcast_to(m, (DEVS, 128))
        weight = jnp.where(m == 0.0, 1.0, 2.0)
        cos, sin = unit(m * lanes.astype(F32))
        step_c, step_s = unit(m * 128.0)
        cos, sin = weight * cos, -weight * sin
        for a in range(HALF // 128):
            at = slice(a * 128, (a + 1) * 128)
            t_hi[0:DEVS, at], t_lo[0:DEVS, at] = split(cos)
            t_hi[DEVS:, at], t_lo[DEVS:, at] = split(sin)
            cos, sin = cos * step_c + sin * step_s, sin * step_c - cos * step_s
        odd = m - 2.0 * jnp.floor(m * 0.5)
        sign = (1.0 - 2.0 * odd).T
        signs.append(jnp.concatenate([sign[0:8], sign[0:8]], axis=1))
    sign_ref[...] = signs[SLOTS - 1]

    for s in range(SLOTS):
        whole = recv.at[s, pl.ds(0, DEVS - 1)]
        pltpu.make_async_copy(whole, whole, recv_sem.at[s]).wait()
        rows = []
        for lt in range(2):
            got = jnp.concatenate([recv[s, :, 2 * r + lt, :] for r in range(2)], axis=0)
            rows.append(got.T)
        w = jnp.concatenate(rows, axis=0)
        if s == SLOTS - 1:
            last_ref[...] = w
        elif s == 0:
            acc_ref[...] = synthesize(w, signs[s], tab_hi[s], tab_lo[s])
        else:
            acc_ref[...] += synthesize(w, signs[s], tab_hi[s], tab_lo[s])
    for s in range(SLOTS):
        whole = send.at[s, pl.ds(0, DEVS - 1)]
        pltpu.make_async_copy(whole, whole, send_sem.at[s]).wait()


def synthesize(w, sign, t_hi, t_lo):
    w_hi, w_lo = split(w)
    sg = sign[0:1].astype(BF16)
    left_hi = jnp.concatenate([w_hi, w_hi * sg], axis=0)
    left_lo = jnp.concatenate([w_lo, w_lo * sg], axis=0)
    return dot(jnp.concatenate([left_hi, left_lo], axis=0), t_hi).reshape(2, 512, HALF).sum(0) + dot(left_hi, t_lo)


def finish_kernel(new_ref, acc_ref, last_ref, sign_ref, last_hi, last_lo, new_hbm, out_hbm, out, new_sem, out_sem):
    for s in range(SLOTS):
        for t in range(TILES):
            pltpu.make_async_copy(
                new_ref.at[s, t], new_hbm.at[s, :, :, :, pl.ds(t * 128, 128)], new_sem.at[s]
            ).start()
    both = acc_ref[...] + synthesize(last_ref[...], sign_ref[...], last_hi[...], last_lo[...])
    for q in range(ROWS):
        for h in range(2):
            base = h * 256 + q * MEMBERS
            out[q, :, h * HALF : (h + 1) * HALF] = both[base : base + MEMBERS, :]
        pltpu.make_async_copy(out.at[q], out_hbm.at[q], out_sem.at[q]).start()
    for q in range(ROWS):
        pltpu.make_async_copy(out.at[q], out_hbm.at[q], out_sem.at[q]).wait()
    for s in range(SLOTS):
        pltpu.make_async_copy(new_ref.at[s], new_ref.at[s], new_sem.at[s]).wait()


def local(coeffs_old, noise, legendre, decay, amplitude, wavenumber_of_slot, lat_order):
    old = coeffs_old.transpose(0, 2, 3, 1, 4)
    fresh = noise.transpose(0, 2, 3, 1, 4)
    vmem = pl.BlockSpec(memory_space=pltpu.VMEM)
    hbm = pl.BlockSpec(memory_space=pltpu.HBM)
    block = (SLOTS, TILES, SCALES, MEMBERS, 2, 128)
    kept = pl.pallas_call(
        exchange_kernel,
        name="exchange",
        out_shape=(
            pltpu.VMEM(block, F32),
            pltpu.VMEM((512, HALF), F32),
            pltpu.VMEM((256, 256), F32),
            pltpu.VMEM((8, 256), F32),
            pltpu.VMEM((2 * DEVS, HALF), BF16),
            pltpu.VMEM((2 * DEVS, HALF), BF16),
        ),
        in_specs=[hbm] * 7,
        out_specs=(vmem,) * 6,
        scratch_shapes=[
            pltpu.VMEM((WIDTH,), jnp.int32),
            pltpu.VMEM((WIDTH,), jnp.int32),
            pltpu.SMEM((WIDTH,), jnp.int32),
            pltpu.SMEM((SCALES,), F32),
            pltpu.VMEM((SCALES, WIDTH), F32),
            pltpu.VMEM(block, F32),
            pltpu.VMEM(block, BF16),
            pltpu.VMEM((SLOTS, WIDTH, WIDTH), F32),
            pltpu.VMEM((TILES, 104, 128), F32),
            pltpu.VMEM((128, WIDTH), F32),
            pltpu.VMEM((WIDTH, WIDTH), BF16),
            pltpu.VMEM((SLOTS, DEVS, 4, 128), F32),
            pltpu.VMEM((SLOTS, DEVS, 4, 128), F32),
            pltpu.VMEM((SLOTS - 1, 2 * DEVS, HALF), BF16),
            pltpu.VMEM((SLOTS - 1, 2 * DEVS, HALF), BF16),
            pltpu.SemaphoreType.DMA((5,)),
            pltpu.SemaphoreType.DMA((2, SLOTS)),
            pltpu.SemaphoreType.DMA((SLOTS,)),
            pltpu.SemaphoreType.DMA((SLOTS,)),
            pltpu.SemaphoreType.DMA((SLOTS,)),
        ],
        compiler_params=pltpu.CompilerParams(collective_id=0, has_side_effects=True, vmem_limit_bytes=44 * 2**20),
    )(*(pltpu.with_memory_space_constraint(v, pltpu.HBM) for v in (lat_order, wavenumber_of_slot, decay, amplitude, old, fresh, legendre)))
    new, pattern = pl.pallas_call(
        finish_kernel,
        name="finish",
        out_shape=(
            jax.ShapeDtypeStruct((SLOTS, SCALES, MEMBERS, 2, WIDTH), F32),
            jax.ShapeDtypeStruct((ROWS, MEMBERS, LON), F32),
        ),
        in_specs=[vmem] * 6,
        out_specs=(hbm, hbm),
        scratch_shapes=[
            pltpu.VMEM((ROWS, MEMBERS, LON), F32),
            pltpu.SemaphoreType.DMA((SLOTS,)),
            pltpu.SemaphoreType.DMA((ROWS,)),
        ],
        compiler_params=pltpu.CompilerParams(vmem_limit_bytes=24 * 2**20),
    )(*kept)
    return new.transpose(0, 3, 1, 2, 4), pattern


def solution(mesh):
    split_slots = P(("lat", "lon"), None, None, None, None)
    in_specs = (split_slots, split_slots, P(("lat", "lon"), None, None), P(), P(), P(), P())
    out_specs = (split_slots, P(("lat", "lon"), None, None))
    return jax.shard_map(local, mesh=mesh, in_specs=in_specs, out_specs=out_specs, check_vma=False)
```

time: 42.3 us -> 33.5 us (0.79)
  Pallas kernels: 37.5 us -> 32.6 us
  local copies, waits for them, and re-layouts: 3.8 us -> 0 us
    pallas_call x2, Pallas kernels: 37.5 us -> 32.6 us  [the longest x1 30 us: local(): pl.pallas_call(exchange_kernel, name='exchange', out_shape=(pltpu.VMEM(bl...]
    unnamed x3 -> x0, local copies, waits for them, and re-layouts: 2.42 us -> none
    reshape x2 -> x0, local copies, waits for them, and re-layouts: 1.38 us -> none  [the longest x1 0.69 us: local(): lat_order.reshape(1, -1)]
where the time goes in v2:
time: 33.5 us; the launch traced here: 33.4 us
  Pallas kernels  32.6 us (97%)
  between operations  0.8 us (2%)
    pallas_call x1, Pallas kernels, local(): pl.pallas_call(exchange_kernel, name='exchange', out_shape=(pltpu.VMEM(bl...  30 us
    pallas_call x1, Pallas kernels, local(): pl.pallas_call(finish_kernel, name='finish', out_shape=(jax.ShapeDtypeStr...  2.61 us

profile of v2, /device:TPU:1, one launch (start us, length us, event | category | flops | bytes accessed | tf_op | source)
XLA Modules:
  0.0 33.4 jit_solution(961164289319219756)
XLA Ops:
  0.6 30.0 %exchange.1 = (f32[5,5,3,50,2,128]{5,4,3,2,1,0:T(2,128)S(1)}, f32[512,640]{1,0:T(8,128)S(1)}, f32[256,256]{1,0:T(8,128)S(1)}, f32[8,256]{1,0:T(8,128)S(1)}, bf16...) custom-call(s32[640]{0:T(1024)} %order_hbm.1, s32[640]{0:T(1024)} %waves_hbm.1, f32[3]{0:T(128)} %decay_hbm.1, ...), custom_call_target="tpu_custom_call" | custom-call | tf_op jit(solution)/shard_map/exchange/pallas_call | solution.py:269
  30.7 2.6 %finish.1 = (f32[5,3,50,2,640]{4,3,2,1,0:T(2,128)}, f32[5,50,1280]{2,1,0:T(8,128)}) custom-call(f32[5,5,3,50,2,128]{5,4,3,2,1,0:T(2,128)S(1)} %get-tuple-element.10.new_ref, f32[512,640]{1,0:T(8,128)S(1)} %get-tuple-element.11.acc_ref, f32[256,256]{1,0:T(8,128)S(1)} %get-tuple-element.12.last_ref, f32[8,256]{1,0:T(8,128)S(1)} %get-tuple-element.13.sign_ref, ...), custom_call_target="tpu_custom_call" | custom-call | tf_op jit(solution)/shard_map/finish/pallas_call | solution.py:306

commit v3 on v2

--- a/solution.py
+++ b/solution.py
@@ -18,6 +18,7 @@
 WIDTH = 640
 SCALES = 3
 TILES = WIDTH // 128
+GROUPS = ((0, 1), (1, 1), (2, 1), (3, 1), (4, 1))
 F32 = jnp.float32
 BF16 = jnp.bfloat16
 
@@ -75,11 +76,6 @@
         px, py, pz = lax.rem(x + dx, 4), lax.rem(y + dy, 4), lax.rem(z + dz, 4)
         pc = lax.rem(c + dc, 2)
         return (px * 4 + py) * 2 + pc, pz
-
-    barrier = pltpu.get_barrier_semaphore()
-    peers = [peer(o) for o in offsets()]
-    for p in peers:
-        pl.semaphore_signal(barrier, inc=1, device_id=p, device_id_type=MESH)
 
     def load(s):
         for t in range(TILES):
@@ -103,17 +99,34 @@
     for copy in small:
         copy.start()
     load(0)
+    barrier = pltpu.get_barrier_semaphore()
+    peers = [peer(o) for o in offsets()]
+    for p in peers:
+        pl.semaphore_signal(barrier, inc=1, device_id=p, device_id_type=MESH)
     load(1)
     for copy in small:
         copy.wait()
 
-    lane = lax.broadcasted_iota(jnp.int32, (DEVS, WIDTH), 1)
-    row = lax.broadcasted_iota(jnp.int32, (DEVS, WIDTH), 0)
-    order = order_ref[...].reshape(1, WIDTH)
+    at_lane = lax.broadcasted_iota(jnp.int32, (8, WIDTH), 1)
+    at_row = lax.broadcasted_iota(jnp.int32, (8, WIDTH), 0)
+    kept = at_lane - ((at_lane * 205) >> 10) * ROWS == at_row
+    parts = []
+    for ref in (order_ref, waves_ref):
+        value = jnp.where(kept, ref[...].reshape(1, WIDTH).astype(F32), 0.0)
+        parts += list(split(value))
+    owner = (lax.broadcasted_iota(jnp.int32, (WIDTH, DEVS), 0) * 205) >> 10
+    owner = jnp.where(owner == lax.broadcasted_iota(jnp.int32, (WIDTH, DEVS), 1), 1.0, 0.0).astype(BF16)
+    picked = jnp.concatenate([p.astype(F32) for p in parts], axis=0).astype(BF16)
+    picked = dot(picked, owner)
+    order_rows = picked[0:8] + picked[8:16]
+    wave_rows = picked[16:24] + picked[24:32]
+
+    spot = lax.broadcasted_iota(jnp.int32, (DEVS, 128), 1).astype(F32)
     for q in range(ROWS):
-        mine = jnp.where(lane == row * ROWS + q, order, 0)
-        shown = jnp.sum(mine.astype(F32), axis=1, keepdims=True).astype(jnp.int32)
-        perm[q * DEVS : (q + 1) * DEVS, :] = jnp.where(lane == shown, 1.0, 0.0).astype(BF16)
+        shown = jnp.broadcast_to(order_rows[q : q + 1], (DEVS, 128)).T
+        for t in range(TILES):
+            hit = jnp.where(spot == shown - 128.0 * t, 1.0, 0.0).astype(BF16)
+            perm[q * DEVS : (q + 1) * DEVS, t * 128 : (t + 1) * 128] = hit
 
     lanes = lax.broadcasted_iota(jnp.int32, (DEVS, 128), 1)
     nt = (((1,), (1,)), ((), ()))
@@ -124,7 +137,7 @@
         pltpu.make_async_copy(old.at[s], old.at[s], load_sem.at[0, s]).wait()
         pltpu.make_async_copy(noise.at[s], noise.at[s], load_sem.at[1, s]).wait()
         wave = wave_ref[me * SLOTS + s]
-        live = lane[0:1] < WIDTH - wave
+        live = at_lane[0:1] < WIDTH - wave
         shifted = pltpu.roll(amp, lax.rem(WIDTH - wave, WIDTH), 1)
         keep, gain = [], []
         for k in range(SCALES):
@@ -152,8 +165,12 @@
             load(s + 2)
         c_hi, c_lo = split(coef[...])
         l_hi, l_lo = split(leg[s])
-        f = dot(l_hi, jnp.concatenate([c_hi, c_lo], axis=0), nt)
-        f = f[:, 0:128] + (f[:, 128:] + dot(l_lo, c_hi, nt))
+        left = jnp.concatenate([l_hi, l_lo], axis=1)
+        right = jnp.concatenate(
+            [jnp.concatenate([c_hi, c_hi], axis=1), jnp.concatenate([c_lo, jnp.zeros_like(c_lo)], axis=1)], axis=0
+        )
+        f = dot(left, right, nt)
+        f = f[:, 0:128] + f[:, 128:]
         f_hi, f_lo = split(f)
         g = dot(perm[...], jnp.concatenate([f_hi, f_lo], axis=1))
         g = g[:, 0:128] + g[:, 128:]
@@ -172,52 +189,65 @@
             send[s, :, 2 * r, :] = low
             send[s, :, 2 * r + 1, :] = high
 
-    def start(s):
+    def start(g):
+        first, count = GROUPS[g]
+        mine = pl.ds(first, count)
         for p in peers:
             pltpu.make_async_remote_copy(
-                src_ref=send.at[s, p[0] * 4 + p[1]],
-                dst_ref=recv.at[s, me],
-                send_sem=send_sem.at[s],
-                recv_sem=recv_sem.at[s],
+                src_ref=send.at[mine, p[0] * 4 + p[1]],
+                dst_ref=recv.at[mine, me],
+                send_sem=send_sem.at[g],
+                recv_sem=recv_sem.at[g],
                 device_id=p,
                 device_id_type=MESH,
             ).start()
-        recv[s, pl.ds(me, 1)] = send[s, pl.ds(me, 1)]
-
-    field(0)
-    pl.semaphore_wait(barrier, DEVS - 1)
-    start(0)
-    for s in range(1, SLOTS):
-        field(s)
-        start(s)
-
-    waves = waves_ref[...].reshape(1, WIDTH)
+        for s in range(first, first + count):
+            recv[s, pl.ds(me, 1)] = send[s, pl.ds(me, 1)]
+
+    for g, (first, count) in enumerate(GROUPS):
+        for s in range(first, first + count):
+            field(s)
+        if g == 0:
+            pl.semaphore_wait(barrier, DEVS - 1)
+        start(g)
+
+    turn = [unit(wave_rows * float(n)) for n in (8, 16, 32, 64, 128)]
+    small_t = lax.broadcasted_iota(jnp.int32, (8, 128), 0).astype(F32)
     signs = []
     for s in range(SLOTS):
         if s < SLOTS - 1:
             t_hi, t_lo = tab_hi.at[s], tab_lo.at[s]
         else:
             t_hi, t_lo = last_hi, last_lo
-        mine = jnp.where(lane == row * SLOTS + s, waves, 0)
-        m = jnp.sum(mine.astype(F32), axis=1, keepdims=True)
-        m = jnp.broadcast_to(m, (DEVS, 128))
+        m = wave_rows[s : s + 1]
         weight = jnp.where(m == 0.0, 1.0, 2.0)
-        cos, sin = unit(m * lanes.astype(F32))
-        step_c, step_s = unit(m * 128.0)
+        cos, sin = unit(jnp.broadcast_to(m, (8, 128)) * small_t)
         cos, sin = weight * cos, -weight * sin
-        for a in range(HALF // 128):
+        for c8, s8 in turn[:4]:
+            c8, s8 = c8[s : s + 1], s8[s : s + 1]
+            cos, sin = (
+                jnp.concatenate([cos, cos * c8 + sin * s8], axis=0),
+                jnp.concatenate([sin, sin * c8 - cos * s8], axis=0),
+            )
+        cos, sin = cos.T, sin.T
+        step_c = jnp.broadcast_to(turn[4][0][s : s + 1], (DEVS, 128)).T
+        step_s = jnp.broadcast_to(turn[4][1][s : s + 1], (DEVS, 128)).T
+        for a in range(TILES):
             at = slice(a * 128, (a + 1) * 128)
             t_hi[0:DEVS, at], t_lo[0:DEVS, at] = split(cos)
             t_hi[DEVS:, at], t_lo[DEVS:, at] = split(sin)
-            cos, sin = cos * step_c + sin * step_s, sin * step_c - cos * step_s
+            if a + 1 < TILES:
+                cos, sin = cos * step_c + sin * step_s, sin * step_c - cos * step_s
         odd = m - 2.0 * jnp.floor(m * 0.5)
-        sign = (1.0 - 2.0 * odd).T
-        signs.append(jnp.concatenate([sign[0:8], sign[0:8]], axis=1))
+        sign = jnp.broadcast_to(1.0 - 2.0 * odd, (8, 128))
+        signs.append(jnp.concatenate([sign, sign], axis=1))
     sign_ref[...] = signs[SLOTS - 1]
 
     for s in range(SLOTS):
-        whole = recv.at[s, pl.ds(0, DEVS - 1)]
-        pltpu.make_async_copy(whole, whole, recv_sem.at[s]).wait()
+        for g, (first, count) in enumerate(GROUPS):
+            if s == first:
+                whole = recv.at[pl.ds(first, count), pl.ds(0, DEVS - 1)]
+                pltpu.make_async_copy(whole, whole, recv_sem.at[g]).wait()
         rows = []
         for lt in range(2):
             got = jnp.concatenate([recv[s, :, 2 * r + lt, :] for r in range(2)], axis=0)
@@ -229,9 +259,9 @@
             acc_ref[...] = synthesize(w, signs[s], tab_hi[s], tab_lo[s])
         else:
             acc_ref[...] += synthesize(w, signs[s], tab_hi[s], tab_lo[s])
-    for s in range(SLOTS):
-        whole = send.at[s, pl.ds(0, DEVS - 1)]
-        pltpu.make_async_copy(whole, whole, send_sem.at[s]).wait()
+    for g, (first, count) in enumerate(GROUPS):
+        whole = send.at[pl.ds(first, count), pl.ds(0, DEVS - 1)]
+        pltpu.make_async_copy(whole, whole, send_sem.at[g]).wait()
 
 
 def synthesize(w, sign, t_hi, t_lo):
@@ -298,8 +328,8 @@
             pltpu.SemaphoreType.DMA((5,)),
             pltpu.SemaphoreType.DMA((2, SLOTS)),
             pltpu.SemaphoreType.DMA((SLOTS,)),
-            pltpu.SemaphoreType.DMA((SLOTS,)),
-            pltpu.SemaphoreType.DMA((SLOTS,)),
+            pltpu.SemaphoreType.DMA((len(GROUPS),)),
+            pltpu.SemaphoreType.DMA((len(GROUPS),)),
         ],
         compiler_params=pltpu.CompilerParams(collective_id=0, has_side_effects=True, vmem_limit_bytes=44 * 2**20),
     )(*(pltpu.with_memory_space_constraint(v, pltpu.HBM) for v in (lat_order, wavenumber_of_slot, decay, amplitude, old, fresh, legendre)))

time: 33.5 us -> 32.5 us (0.970)
  Pallas kernels: 32.6 us -> 31.6 us
    pallas_call x1, Pallas kernels: 30 us -> 29 us  [local(): pl.pallas_call(exchange_kernel, name='exchange', out_shape=(pltpu.VMEM(bl...]
where the time goes in v3:
time: 32.5 us; the launch traced here: 32.4 us
  Pallas kernels  31.6 us (97%)
  between operations  0.8 us (2%)
    pallas_call x1, Pallas kernels, local(): pl.pallas_call(exchange_kernel, name='exchange', out_shape=(pltpu.VMEM(bl...  29 us
    pallas_call x1, Pallas kernels, local(): pl.pallas_call(finish_kernel, name='finish', out_shape=(jax.ShapeDtypeStr...  2.61 us

profile of v3, /device:TPU:1, one launch (start us, length us, event | category | flops | bytes accessed | tf_op | source)
XLA Modules:
  0.0 32.4 jit_solution(3493852442321186504)
XLA Ops:
  0.6 29.0 %exchange.1 = (f32[5,5,3,50,2,128]{5,4,3,2,1,0:T(2,128)S(1)}, f32[512,640]{1,0:T(8,128)S(1)}, f32[256,256]{1,0:T(8,128)S(1)}, f32[8,256]{1,0:T(8,128)S(1)}, bf16...) custom-call(s32[640]{0:T(1024)} %order_hbm.1, s32[640]{0:T(1024)} %waves_hbm.1, f32[3]{0:T(128)} %decay_hbm.1, ...), custom_call_target="tpu_custom_call" | custom-call | tf_op jit(solution)/shard_map/exchange/pallas_call | solution.py:299
  29.6 2.6 %finish.1 = (f32[5,3,50,2,640]{4,3,2,1,0:T(2,128)}, f32[5,50,1280]{2,1,0:T(8,128)}) custom-call(f32[5,5,3,50,2,128]{5,4,3,2,1,0:T(2,128)S(1)} %get-tuple-element.10.new_ref, f32[512,640]{1,0:T(8,128)S(1)} %get-tuple-element.11.acc_ref, f32[256,256]{1,0:T(8,128)S(1)} %get-tuple-element.12.last_ref, f32[8,256]{1,0:T(8,128)S(1)} %get-tuple-element.13.sign_ref, ...), custom_call_target="tpu_custom_call" | custom-call | tf_op jit(solution)/shard_map/finish/pallas_call | solution.py:336

commit v4 on v3

--- a/solution.py
+++ b/solution.py
@@ -77,11 +77,15 @@
         pc = lax.rem(c + dc, 2)
         return (px * 4 + py) * 2 + pc, pz
 
+    noise_rows = noise_hbm.reshape(SLOTS, SCALES, 2 * MEMBERS, WIDTH)
+
     def load(s):
         for t in range(TILES):
             lanes_of = pl.ds(t * 128, 128)
             pltpu.make_async_copy(old_hbm.at[s, :, :, :, lanes_of], old.at[s, t], load_sem.at[0, s]).start()
-            pltpu.make_async_copy(noise_hbm.at[s, :, :, :, lanes_of], noise.at[s, t], load_sem.at[1, s]).start()
+            pltpu.make_async_copy(
+                noise_rows.at[s, :, :, lanes_of], noise.at[s, t, :, 0 : 2 * MEMBERS], load_sem.at[1, s]
+            ).start()
         pltpu.make_async_copy(leg_hbm.at[s], leg.at[s], leg_sem.at[s]).start()
 
     small = [
@@ -135,7 +139,8 @@
 
     def advance(s):
         pltpu.make_async_copy(old.at[s], old.at[s], load_sem.at[0, s]).wait()
-        pltpu.make_async_copy(noise.at[s], noise.at[s], load_sem.at[1, s]).wait()
+        whole = noise.at[s, :, :, 0 : 2 * MEMBERS]
+        pltpu.make_async_copy(whole, whole, load_sem.at[1, s]).wait()
         wave = wave_ref[me * SLOTS + s]
         live = at_lane[0:1] < WIDTH - wave
         shifted = pltpu.roll(amp, lax.rem(WIDTH - wave, WIDTH), 1)
@@ -150,7 +155,7 @@
             for k in range(SCALES):
                 fresh = (
                     keep[k][:, at] * old.at[s, t, k].reshape(2 * MEMBERS, 128)[...]
-                    + gain[k][:, at] * noise.at[s, t, k].reshape(2 * MEMBERS, 128)[...].astype(F32)
+                    + gain[k][:, at] * noise[s, t, k, 0 : 2 * MEMBERS, :].astype(F32)
                 )
                 new_ref.at[s, t, k].reshape(2 * MEMBERS, 128)[...] = fresh
                 summed = fresh if summed is None else summed + fresh
@@ -316,7 +321,7 @@
             pltpu.SMEM((SCALES,), F32),
             pltpu.VMEM((SCALES, WIDTH), F32),
             pltpu.VMEM(block, F32),
-            pltpu.VMEM(block, BF16),
+            pltpu.VMEM((SLOTS, TILES, SCALES, 112, 128), BF16),
             pltpu.VMEM((SLOTS, WIDTH, WIDTH), F32),
             pltpu.VMEM((TILES, 104, 128), F32),
             pltpu.VMEM((128, WIDTH), F32),

time: 32.5 us -> 31.7 us (0.975)
  Pallas kernels: 31.6 us -> 30.8 us
    pallas_call x1, Pallas kernels: 29 us -> 28.2 us  [local(): pl.pallas_call(exchange_kernel, name='exchange', out_shape=(pltpu.VMEM(bl...]
where the time goes in v4:
time: 31.7 us; the launch traced here: 31.6 us
  Pallas kernels  30.8 us (97%)
  between operations  0.8 us (3%)
    pallas_call x1, Pallas kernels, local(): pl.pallas_call(exchange_kernel, name='exchange', out_shape=(pltpu.VMEM(bl...  28.2 us
    pallas_call x1, Pallas kernels, local(): pl.pallas_call(finish_kernel, name='finish', out_shape=(jax.ShapeDtypeStr...  2.62 us

profile of v4, /device:TPU:1, one launch (start us, length us, event | category | flops | bytes accessed | tf_op | source)
XLA Modules:
  0.0 31.6 jit_solution(4507118998986934712)
XLA Ops:
  0.6 28.2 %exchange.1 = (f32[5,5,3,50,2,128]{5,4,3,2,1,0:T(2,128)S(1)}, f32[512,640]{1,0:T(8,128)S(1)}, f32[256,256]{1,0:T(8,128)S(1)}, f32[8,256]{1,0:T(8,128)S(1)}, bf16...) custom-call(s32[640]{0:T(1024)} %order_hbm.1, s32[640]{0:T(1024)} %waves_hbm.1, f32[3]{0:T(128)} %decay_hbm.1, ...), custom_call_target="tpu_custom_call" | custom-call | tf_op jit(solution)/shard_map/exchange/pallas_call | solution.py:304
  28.8 2.6 %finish.1 = (f32[5,3,50,2,640]{4,3,2,1,0:T(2,128)}, f32[5,50,1280]{2,1,0:T(8,128)}) custom-call(f32[5,5,3,50,2,128]{5,4,3,2,1,0:T(2,128)S(1)} %get-tuple-element.10.new_ref, f32[512,640]{1,0:T(8,128)S(1)} %get-tuple-element.11.acc_ref, f32[256,256]{1,0:T(8,128)S(1)} %get-tuple-element.12.last_ref, f32[8,256]{1,0:T(8,128)S(1)} %get-tuple-element.13.sign_ref, ...), custom_call_target="tpu_custom_call" | custom-call | tf_op jit(solution)/shard_map/finish/pallas_call | solution.py:341

commit v5 on v4

--- a/solution.py
+++ b/solution.py
@@ -170,12 +170,8 @@
             load(s + 2)
         c_hi, c_lo = split(coef[...])
         l_hi, l_lo = split(leg[s])
-        left = jnp.concatenate([l_hi, l_lo], axis=1)
-        right = jnp.concatenate(
-            [jnp.concatenate([c_hi, c_hi], axis=1), jnp.concatenate([c_lo, jnp.zeros_like(c_lo)], axis=1)], axis=0
-        )
-        f = dot(left, right, nt)
-        f = f[:, 0:128] + f[:, 128:]
+        f = dot(l_hi, jnp.concatenate([c_hi, c_lo], axis=0), nt)
+        f = f[:, 0:128] + (f[:, 128:] + dot(l_lo, c_hi, nt))
         f_hi, f_lo = split(f)
         g = dot(perm[...], jnp.concatenate([f_hi, f_lo], axis=1))
         g = g[:, 0:128] + g[:, 128:]

time: 31.7 us -> 31.2 us (0.984)
  Pallas kernels: 30.8 us -> 30.2 us
    pallas_call x1, Pallas kernels: 28.2 us -> 27.6 us  [local(): pl.pallas_call(exchange_kernel, name='exchange', out_shape=(pltpu.VMEM(bl...]
where the time goes in v5:
time: 31.2 us; the launch traced here: 31 us
  Pallas kernels  30.2 us (97%)
  between operations  0.8 us (3%)
    pallas_call x1, Pallas kernels, local(): pl.pallas_call(exchange_kernel, name='exchange', out_shape=(pltpu.VMEM(bl...  27.6 us
    pallas_call x1, Pallas kernels, local(): pl.pallas_call(finish_kernel, name='finish', out_shape=(jax.ShapeDtypeStr...  2.62 us

profile of v5, /device:TPU:1, one launch (start us, length us, event | category | flops | bytes accessed | tf_op | source)
XLA Modules:
  0.0 31.0 jit_solution(9216275528866445647)
XLA Ops:
  0.6 27.6 %exchange.1 = (f32[5,5,3,50,2,128]{5,4,3,2,1,0:T(2,128)S(1)}, f32[512,640]{1,0:T(8,128)S(1)}, f32[256,256]{1,0:T(8,128)S(1)}, f32[8,256]{1,0:T(8,128)S(1)}, bf16...) custom-call(s32[640]{0:T(1024)} %order_hbm.1, s32[640]{0:T(1024)} %waves_hbm.1, f32[3]{0:T(128)} %decay_hbm.1, ...), custom_call_target="tpu_custom_call" | custom-call | tf_op jit(solution)/shard_map/exchange/pallas_call | solution.py:300
  28.2 2.6 %finish.1 = (f32[5,3,50,2,640]{4,3,2,1,0:T(2,128)}, f32[5,50,1280]{2,1,0:T(8,128)}) custom-call(f32[5,5,3,50,2,128]{5,4,3,2,1,0:T(2,128)S(1)} %get-tuple-element.10.new_ref, f32[512,640]{1,0:T(8,128)S(1)} %get-tuple-element.11.acc_ref, f32[256,256]{1,0:T(8,128)S(1)} %get-tuple-element.12.last_ref, f32[8,256]{1,0:T(8,128)S(1)} %get-tuple-element.13.sign_ref, ...), custom_call_target="tpu_custom_call" | custom-call | tf_op jit(solution)/shard_map/finish/pallas_call | solution.py:337
